TPU v7x, 32 devices: a whole 2x2x4 slice. The times are simulated.
32 devices in a mesh: dp: 2 (over x), expert: 16 (over z, y, core).
Axes of the slice: x: 2, y: 2, z: 4, core: 2. Of those that a mesh axis runs over, the one named last changes fastest.
Arguments:
- tokens: bfloat16 [32, 256, 1280], P(('dp', 'expert')), may hold values from -12 to 12
- router: bfloat16 [1280, 16], replicated, may hold values from -3 to 3
- w_in: bfloat16 [16, 1280, 5120], P('expert', None, 'dp'), may hold values from -0.15625 to 0.15625
- b_in: bfloat16 [16, 5120], P('expert'), may hold values from -3 to 3
- w_out: bfloat16 [16, 5120, 1280], P('expert', 'dp'), may hold values from -0.078125 to 0.078125
- b_out: bfloat16 [16, 1280], P('expert'), may hold values from -3 to 3
Outputs:
- mixed: bfloat16 [32, 256, 1280], P(('dp', 'expert'))
All inputs are finite; a program needn't handle non-finite values.
Results may differ from a plain program's by a relative error of at most 0.014.
Values may be sent and summed in bfloat16 or wider, within the bound.
A program may use at most 64 MiB of HBM per device.

v0:
```python
import jax
import jax.numpy as jnp
from jax import lax
from jax.sharding import PartitionSpec as P


def shards(tokens, router, w_in, b_in, w_out, b_out):
    logits = jnp.einsum("bmd,de->bme", tokens, router, preferred_element_type=jnp.float32)
    dispatch = jax.nn.softmax(logits, axis=1).astype(jnp.bfloat16)
    combine = jax.nn.softmax(logits, axis=2).astype(jnp.bfloat16)
    slot_inputs = jnp.einsum(
        "bme,bmd->ebd", dispatch, tokens, preferred_element_type=jnp.float32
    ).astype(jnp.bfloat16)
    width = tokens.shape[2]
    arrived = lax.all_to_all(slot_inputs, "expert", split_axis=0, concat_axis=0, tiled=True)
    sources = arrived.shape[0]
    images = arrived.shape[1]
    paired = lax.all_gather(arrived, "dp", axis=0, tiled=True)
    flat = paired.reshape(paired.shape[0] * images, width)
    half = w_in.shape[2]
    offset = lax.axis_index("dp") * half
    bias_half = lax.dynamic_slice_in_dim(b_in[0], offset, half, 0).astype(jnp.float32)
    hidden = jax.nn.gelu(
        jnp.dot(flat, w_in[0], preferred_element_type=jnp.float32) + bias_half, approximate=False
    ).astype(jnp.bfloat16)
    summed = lax.psum_scatter(
        jnp.dot(hidden, w_out[0], preferred_element_type=jnp.float32).astype(jnp.bfloat16),
        "dp",
        scatter_dimension=0,
        tiled=True,
    ).astype(jnp.float32)
    result = (summed + b_out[0].astype(jnp.float32)).astype(jnp.bfloat16)
    shaped = result.reshape(sources, images, width)
    returned = lax.all_to_all(shaped, "expert", split_axis=0, concat_axis=0, tiled=True)
    mixed = jnp.einsum("bme,ebd->bmd", combine, returned, preferred_element_type=jnp.float32)
    return mixed.astype(jnp.bfloat16)


def solution(mesh):
    return jax.shard_map(
        shards,
        mesh=mesh,
        in_specs=(
            P(("dp", "expert"), None, None),
            P(),
            P("expert", None, "dp"),
            P("expert", None),
            P("expert", "dp", None),
            P("expert", None),
        ),
        out_specs=P(("dp", "expert"), None, None),
        check_vma=False,
    )
```

profile of v0, /device:TPU:0, one launch (start us, length us, event | category | flops | bytes accessed | tf_op | source)
XLA Modules:
  0.0 67.4 jit_solution(4373061189668282415)
XLA Ops:
  6.5 0.0 copy-start
  6.5 1.1 %copy-done = bf16[1,256,1280]{2,1,0:T(8,128)(2,1)S(1)} copy-done((bf16[1,256,1280]{2,1,0:T(8,128)(2,1)S(1)}, bf16[1,256,1280]{2,1,0:T(8,128)(2,1)}, u32[]{:S(2)}) %copy-start) | copy-done | bytes 655384
  7.6 1.2 %fusion.101 = (f32[256]{0:T(256)S(1)}, f32[16]{0:T(128)S(1)}, f32[256,16]{0,1:T(8,128)S(1)}) fusion(bf16[1280,16]{0,1:T(8,128)(2,1)} %param.7, bf16[1,256,1280]{2,1,0:T(8,128)(2,1)S(1)} %copy-done), kind=kOutput, calls=%fused_computation.110 | convolution fusion | flops 10493680 | bytes 713792 | tf_op jit(solution)/shard_map/bmd,de->bme/dot_general | solution.py:8
  8.8 0.2 fusion.65
  9.0 0.3 fusion.11
  9.3 0.6 broadcast.23
  9.9 0.6 reduce.12
  10.5 0.6 reshape.59
  11.2 7.4 %all-to-all-start = ((bf16[16,2,640]{2,1,0:T(2,128)(2,1)}), bf16[16,2,640]{2,1,0:T(2,128)(2,1)S(1)}, u32[]{:S(2)}, u32[]{:S(2)}) async-start(bf16[16,2,640]{2,1,0:T(2,128)(2,1)} %reshape.59), calls=%async_computation | async-start | bytes 81920 | tf_op jit(solution)/shard_map/all_to_all | solution.py:15
  18.6 0.0 reduce-scatter.2.cloned.1.call-start
  18.6 0.7 %convert_reduce_fusion = f32[2560]{0:T(1024)S(1)} fusion(bf16[1,5120]{1,0:T(2,128)(2,1)} %param.9, s32[]{:T(128)S(6)} %select_n.3), kind=kLoop, calls=%fused_computation.74 | loop fusion | flops 2560 | bytes 15364 | tf_op jit(solution)/shard_map/add | solution.py:24
  19.4 5.9 %all-to-all-done = bf16[16,2,640]{2,1,0:T(2,128)(2,1)S(1)} async-done(((bf16[16,2,640]{2,1,0:T(2,128)(2,1)}), bf16[16,2,640]{2,1,0:T(2,128)(2,1)S(1)}, u32[]{:S(2)}, u32[]{:S(2)}) %all-to-all-start) | async-done | bytes 40992 | tf_op jit(solution)/shard_map/all_to_all | solution.py:15
  25.3 4.7 %all_gather.3 = bf16[32,1,1280]{2,0,1:T(8,128)(2,1)S(1)} all-gather(bf16[16,1,1280]{2,0,1:T(8,128)(2,1)S(1)} %copy.10), channel_id=1, replica_groups=mesh['dp'=2,'expert'=16] {'dp'}, dimensions={0}, use_global_device_ids=true | all-gather | bytes 122880 | tf_op jit(solution)/shard_map/all_gather | solution.py:18
  30.0 0.0 copy-start.1
  30.0 8.2 %fusion.8 = bf16[32,1280]{1,0:T(8,128)(2,1)} fusion(bf16[1,2560,1280]{2,1,0:T(8,128)(2,1)} %param.10, bf16[1,1280,2560]{2,1,0:T(8,128)(2,1)} %param.8, f32[2560]{0:T(1024)S(1)} %convert_reduce_fusion, bf16[32,1,1280]{2,0,1:T(8,128)(2,1)S(1)} %all_gather.3), kind=kOutput, calls=%fused_computation.7 | convolution fusion | flops 424878080 | bytes 13281280 | tf_op jit(solution)/shard_map/dot_general | solution.py:27
  38.2 0.0 reduce-scatter.2.cloned.1.call-update
  38.2 0.0 copy-done.1
  38.3 7.4 %reduce-scatter.2.cloned.1.call-done = bf16[16,1280]{1,0:T(8,128)(2,1)} async-done(((bf16[32,1280]{1,0:T(8,128)(2,1)}), bf16[16,1280]{1,0:T(8,128)(2,1)}) %reduce-scatter.2.cloned.1.call-update) | async-done | bytes 40976 | tf_op jit(solution)/shard_map/reduce_scatter | solution.py:26
  45.7 0.8 %fusion.62 = bf16[16,1,1280]{2,0,1:T(8,128)(2,1)S(1)} fusion(bf16[16,1280]{1,0:T(8,128)(2,1)} %reduce-scatter.2.cloned.1.call-done, f32[1280]{0:T(1024)S(1)} %convert_reduce_fusion.1), kind=kLoop, calls=%fused_computation.65 | loop fusion | flops 61440 | bytes 87040 | tf_op jit(solution)/shard_map/reshape | solution.py:33
  46.5 0.6 reduce.13
  47.2 12.1 %all_to_all.10 = bf16[16,2,640]{2,1,0:T(2,128)(2,1)S(1)} all-to-all(bf16[16,2,640]{2,1,0:T(2,128)(2,1)S(1)} %reshape.61), channel_id=1, replica_groups=mesh['dp'=2,'expert'=16] {'expert'}, dimensions={0} | all-to-all | bytes 81920 | tf_op jit(solution)/shard_map/all_to_all | solution.py:34
  59.3 1.2 %fusion.7 = bf16[1,256,1280]{2,1,0:T(8,128)(2,1)} fusion(bf16[16,1,1280]{2,1,0:T(2,128)(2,1)S(1)} %reshape.62, f32[256,16]{0,1:T(8,128)S(1)} %get-tuple-element.9, f32[256]{0:T(256)S(1)} %get-tuple-element.5, f32[256]{0:T(256)S(1)} %get-tuple-element.7), kind=kOutput, calls=%fused_computation.6 | convolution fusion | flops 10825728 | bytes 714752 | tf_op jit(solution)/shard_map/bme,ebd->bmd/dot_general | solution.py:35
  (5 shorter events, 0.1 us)
Async XLA Ops:
  6.5 1.1 %copy-start = (bf16[1,256,1280]{2,1,0:T(8,128)(2,1)S(1)}, bf16[1,256,1280]{2,1,0:T(8,128)(2,1)}, u32[]{:S(2)}) copy-start(bf16[1,256,1280]{2,1,0:T(8,128)(2,1)} %param.6) | copy-start | bytes 1966084
  11.2 14.1 %all-to-all-start = ((bf16[16,2,640]{2,1,0:T(2,128)(2,1)}), bf16[16,2,640]{2,1,0:T(2,128)(2,1)S(1)}, u32[]{:S(2)}, u32[]{:S(2)}) async-start(bf16[16,2,640]{2,1,0:T(2,128)(2,1)} %reshape.59), calls=%async_computation | async-start | bytes 81920 | tf_op jit(solution)/shard_map/all_to_all | solution.py:15
  18.6 27.1 %reduce-scatter.2.cloned.1.call-start = ((), (), s32[]{:S(2)}) async-start(), calls=%async_computation.3 | async-start | bytes 122880 | tf_op jit(solution)/shard_map/reduce_scatter | solution.py:26
  30.0 8.2 %copy-start.1 = (bf16[1,1280]{1,0:T(2,128)(2,1)S(1)}, bf16[1,1280]{1,0:T(2,128)(2,1)}, u32[]{:S(2)}) copy-start(bf16[1,1280]{1,0:T(2,128)(2,1)} %param.11) | copy-start | bytes 7684
Sparse Core Ops, SparseCore 0:
  38.4 7.3 reduce-scatter.1
where the time goes:
time: 67.8 us; the launch traced here: 67.4 us
  blocking collectives  16.8 us (25%)
  between operations  13.5 us (20%)
  waiting for transfers between devices  13.4 us (20%)
  matrix products  10.9 us (16%)
  starting transfers between devices  7.45 us (11%)
  other arithmetic  3.02 us (4%)
  local copies, waits for them, and re-layouts  2.41 us (4%)
    all_to_all x1, blocking collectives, shards(): lax.all_to_all(shaped, 'expert', split_axis=0, concat_axis=0, tiled=True)  12.1 us
    dot_general x1, matrix products, shards(): jnp.dot(hidden, w_out[0], preferred_element_type=jnp.float32)  8.21 us
    reduce_scatter x1, waiting for transfers between devices, shards(): lax.psum_scatter(jnp.dot(hidden, w_out[0], preferred_element_type=jnp.flo...  7.44 us
    all_to_all x1, starting transfers between devices, shards(): lax.all_to_all(slot_inputs, 'expert', split_axis=0, concat_axis=0, tiled=...  7.41 us
    all_to_all x1, waiting for transfers between devices, shards(): lax.all_to_all(slot_inputs, 'expert', split_axis=0, concat_axis=0, tiled=...  5.91 us
    all_gather x1, blocking collectives, shards(): paired = lax.all_gather(arrived, 'dp', axis=0, tiled=True)  4.67 us
    unnamed x8, local copies, waits for them, and re-layouts  1.81 us
    reshape x2, other arithmetic, shards(): shaped = result.reshape(sources, images, width)  1.43 us
  transfers between devices with their start and end apart: 2, of which 2 were waited for; matrix products, arithmetic and copies ran while one was open for 1% of the time, Pallas kernels for 0%

commit v1 on v0

v1 whole, which is shorter than its diff:
```python
import functools

import jax
import jax.numpy as jnp
from jax import lax
from jax.experimental import pallas as pl
from jax.experimental.pallas import tpu as pltpu
from jax.sharding import PartitionSpec as P

MESH = pl.DeviceIdType.MESH
LANES = 128
SUBLANES = 16


def gelu(v):
    return v * (1.0 + lax.erf(v * (0.5**0.5))) * 0.5


def exchange(n, n_ex, me, source, row_of, landing, send_sem, recv_sem):
    def step(k, carry):
        dest = lax.rem(me + k, n)
        pltpu.make_async_remote_copy(
            src_ref=source.at[row_of(dest)],
            dst_ref=landing.at[me],
            send_sem=send_sem,
            recv_sem=recv_sem,
            device_id=(dest // n_ex, lax.rem(dest, n_ex)),
            device_id_type=MESH,
        ).start()
        return carry

    lax.fori_loop(1, n, step, 0)
    landing[me] = source[row_of(me)]


def wait_bytes(buffer, count, sem):
    rows = buffer.at[pl.ds(0, count)]
    pltpu.make_async_copy(rows, rows, sem).wait()


def kernel(
    n_dp,
    n_ex,
    tokens_hbm,
    router_hbm,
    w_in_hbm,
    b_in_hbm,
    w_out_hbm,
    b_out_hbm,
    out_ref,
    tok,
    router,
    w_in,
    b_in,
    w_out,
    b_out,
    wide_slots,
    wide_rows,
    send1,
    recv1,
    send2,
    recv2,
    x_ref,
    hid,
    comb_ref,
    eo,
    load_sems,
    w_in_sems,
    w_out_sems,
    send_sems,
    recv_sems,
):
    n = n_dp * n_ex
    me_dp = lax.axis_index("dp")
    me_ex = lax.axis_index("expert")
    me = me_dp * n_ex + me_ex
    width = tok.shape[1]
    chunks = width // LANES
    pitch = send1.shape[1]

    loads = [
        pltpu.make_async_copy(tokens_hbm.at[0], tok, load_sems.at[0]),
        pltpu.make_async_copy(router_hbm, router, load_sems.at[1]),
        pltpu.make_async_copy(b_in_hbm, b_in, load_sems.at[2]),
        pltpu.make_async_copy(b_out_hbm, b_out, load_sems.at[3]),
    ]
    for load in loads:
        load.start()

    barrier = pltpu.get_barrier_semaphore()

    def greet(k, carry):
        dest = lax.rem(me + k, n)
        pl.semaphore_signal(
            barrier, inc=1, device_id=(dest // n_ex, lax.rem(dest, n_ex)), device_id_type=MESH
        )
        return carry

    lax.fori_loop(1, n, greet, 0)

    def pieces(hbm, vmem, sems):
        count = sems.shape[0]
        rows = vmem.shape[0] // count
        return [
            pltpu.make_async_copy(
                hbm.at[0, pl.ds(i * rows, rows)], vmem.at[pl.ds(i * rows, rows)], sems.at[i]
            )
            for i in range(count)
        ]

    w_in_loads = pieces(w_in_hbm, w_in, w_in_sems)
    w_out_loads = pieces(w_out_hbm, w_out, w_out_sems)
    for load in w_in_loads + w_out_loads:
        load.start()

    loads[0].wait()
    loads[1].wait()
    logits = lax.dot_general(
        router[...], tok[...], (((1,), (1,)), ((), ())), preferred_element_type=jnp.float32
    )
    over_tokens = jnp.exp(logits - jnp.max(logits, axis=1, keepdims=True))
    dispatch = (over_tokens / jnp.sum(over_tokens, axis=1, keepdims=True)).astype(jnp.bfloat16)
    slots = jnp.dot(dispatch, tok[...], preferred_element_type=jnp.float32)
    for j in range(chunks):
        wide_slots[pl.ds(j, n_ex, stride=pitch), :] = slots[:, j * LANES : (j + 1) * LANES]
    send1[...] = wide_slots[...].reshape(send1.shape).astype(jnp.bfloat16)

    pl.semaphore_wait(barrier, n - 1)
    exchange(n, n_ex, me, send1, lambda d: lax.rem(d, n_ex), recv1, send_sems.at[0], recv_sems.at[0])

    over_experts = jnp.exp(logits - jnp.max(logits, axis=0, keepdims=True))
    combine = over_experts / jnp.sum(over_experts, axis=0, keepdims=True)
    comb_ref[...] = combine.astype(jnp.bfloat16)

    for load in loads[2:] + w_in_loads:
        load.wait()
    wait_bytes(recv1, n - 1, recv_sems.at[0])
    wide_rows[...] = recv1[...].astype(jnp.float32).reshape(wide_rows.shape)
    for j in range(chunks):
        x_ref[:, j * LANES : (j + 1) * LANES] = wide_rows[pl.ds(j, n, stride=pitch), :].astype(jnp.bfloat16)

    half = w_in.shape[1]
    tile = 2 * LANES

    @pl.loop(0, half // tile)
    def _(t):
        at = pl.multiple_of(t * tile, tile)
        bias = b_in[:, pl.ds(pl.multiple_of(me_dp * half + at, LANES), tile)].astype(jnp.float32)
        v = jnp.dot(x_ref[...], w_in[:, pl.ds(at, tile)], preferred_element_type=jnp.float32) + bias
        hid[:, pl.ds(at, tile)] = gelu(v).astype(jnp.bfloat16)

    for load in w_out_loads:
        load.wait()
    keep = (me_dp == 0).astype(jnp.float32)
    for at in range(0, width, tile):
        y = jnp.dot(hid[...], w_out[:, at : at + tile], preferred_element_type=jnp.float32)
        y = y + keep * b_out[:, at : at + tile].astype(jnp.float32)
        for c in range(tile // LANES):
            wide_rows[pl.ds(at // LANES + c, n, stride=pitch), :] = y[:, c * LANES : (c + 1) * LANES]
    send2[...] = wide_rows[...].reshape(send2.shape).astype(jnp.bfloat16)

    exchange(n, n_ex, me, send2, lambda d: d, recv2, send_sems.at[1], recv_sems.at[1])
    wait_bytes(recv2, n - 1, recv_sems.at[1])
    wide_rows[...] = recv2[...].astype(jnp.float32).reshape(wide_rows.shape)
    for j in range(chunks):
        total = wide_rows[pl.ds(j, n_ex, stride=pitch), :]
        for a in range(1, n_dp):
            total = total + wide_rows[pl.ds(a * n_ex * pitch + j, n_ex, stride=pitch), :]
        eo[:, j * LANES : (j + 1) * LANES] = total.astype(jnp.bfloat16)
    mixed = lax.dot_general(
        comb_ref[...], eo[...], (((0,), (0,)), ((), ())), preferred_element_type=jnp.float32
    )
    out_ref[0] = mixed.astype(jnp.bfloat16)
    wait_bytes(recv1, n - 1, send_sems.at[0])
    wait_bytes(recv2, n - 1, send_sems.at[1])


def shards(n_dp, n_ex, tokens, router, w_in, b_in, w_out, b_out):
    n = n_dp * n_ex
    images, m, width = tokens.shape
    assert images == 1 and w_in.shape[0] == 1
    half = w_in.shape[2]
    chunks = width // LANES
    pitch = -(-chunks // SUBLANES) * SUBLANES
    bf16, f32 = jnp.bfloat16, jnp.float32
    return pl.pallas_call(
        functools.partial(kernel, n_dp, n_ex),
        out_shape=jax.ShapeDtypeStruct(tokens.shape, bf16),
        in_specs=[pl.BlockSpec(memory_space=pltpu.HBM)] * 6,
        out_specs=pl.BlockSpec(memory_space=pltpu.VMEM),
        scratch_shapes=[
            pltpu.VMEM((m, width), bf16),
            pltpu.VMEM(router.shape[::-1], bf16),
            pltpu.VMEM(w_in.shape[1:], bf16),
            pltpu.VMEM(b_in.shape, bf16),
            pltpu.VMEM(w_out.shape[1:], bf16),
            pltpu.VMEM(b_out.shape, bf16),
            pltpu.VMEM((n_ex * pitch, LANES), f32),
            pltpu.VMEM((n * pitch, LANES), f32),
            pltpu.VMEM((n_ex, pitch, LANES), bf16),
            pltpu.VMEM((n, pitch, LANES), bf16),
            pltpu.VMEM((n, pitch, LANES), bf16),
            pltpu.VMEM((n, pitch, LANES), bf16),
            pltpu.VMEM((n, width), bf16),
            pltpu.VMEM((n, half), bf16),
            pltpu.VMEM((n_ex, m), bf16),
            pltpu.VMEM((n_ex, width), bf16),
            pltpu.SemaphoreType.DMA((4,)),
            pltpu.SemaphoreType.DMA((4,)),
            pltpu.SemaphoreType.DMA((4,)),
            pltpu.SemaphoreType.DMA((2,)),
            pltpu.SemaphoreType.DMA((2,)),
        ],
        compiler_params=pltpu.CompilerParams(
            collective_id=0, has_side_effects=True, vmem_limit_bytes=60 * 1024 * 1024
        ),
    )(tokens, router.T, w_in, b_in, w_out, b_out)


def solution(mesh):
    return jax.shard_map(
        functools.partial(shards, mesh.shape["dp"], mesh.shape["expert"]),
        mesh=mesh,
        in_specs=(
            P(("dp", "expert"), None, None),
            P(),
            P("expert", None, "dp"),
            P("expert", None),
            P("expert", "dp", None),
            P("expert", None),
        ),
        out_specs=P(("dp", "expert"), None, None),
        check_vma=False,
    )
```

time: 67.8 us -> 25.2 us (0.37)
  Pallas kernels: 0 us -> 23.1 us
  blocking collectives: 16.8 us -> 0 us
  between operations: 13.5 us -> 0.01 us
  waiting for transfers between devices: 13.4 us -> 0 us
  matrix products: 10.9 us -> 0 us
  starting transfers between devices: 7.45 us -> 0 us
  other arithmetic: 3.02 us -> 0 us
    pallas_call x0 -> x1, Pallas kernels: none -> 23.1 us  [shards(): pl.pallas_call(functools.partial(kernel, n_dp, n_ex), out_shape=jax.Shape...]
    all_to_all x1 -> x0, blocking collectives: 12.1 us -> none  [shards(): lax.all_to_all(shaped, 'expert', split_axis=0, concat_axis=0, tiled=True)]
    dot_general x4 -> x0, matrix products: 10.9 us -> none  [the longest x1 8.21 us: shards(): jnp.dot(hidden, w_out[0], preferred_element_type=jnp.float32)]
    reduce_scatter x1 -> x0, waiting for transfers between devices: 7.44 us -> none  [shards(): lax.psum_scatter(jnp.dot(hidden, w_out[0], preferred_element_type=jnp.flo...]
    all_to_all x1 -> x0, starting transfers between devices: 7.41 us -> none  [shards(): lax.all_to_all(slot_inputs, 'expert', split_axis=0, concat_axis=0, tiled=...]
    all_to_all x1 -> x0, waiting for transfers between devices: 5.91 us -> none  [shards(): lax.all_to_all(slot_inputs, 'expert', split_axis=0, concat_axis=0, tiled=...]
    all_gather x1 -> x0, blocking collectives: 4.67 us -> none  [shards(): paired = lax.all_gather(arrived, 'dp', axis=0, tiled=True)]
    reshape x2 -> x0, other arithmetic: 1.43 us -> none  [shards(): shaped = result.reshape(sources, images, width)]
  transfers between devices with their start and end apart: 2 -> 0, of which waited for: 2 -> 0; matrix products, arithmetic and copies ran while one was open for 1% -> 0% of each run, Pallas kernels for 0% -> 0%
where the time goes in v1:
time: 25.2 us; the launch traced here: 25.1 us
  Pallas kernels  23.1 us (92%)
  local copies, waits for them, and re-layouts  1.97 us (8%)
    pallas_call x1, Pallas kernels, shards(): pl.pallas_call(functools.partial(kernel, n_dp, n_ex), out_shape=jax.Shape...  23.1 us
    unnamed x1, local copies, waits for them, and re-layouts  1.97 us

profile of v1, /device:TPU:0, one launch (start us, length us, event | category | flops | bytes accessed | tf_op | source)
XLA Modules:
  0.0 25.1 jit_solution(9063844189950842348)
XLA Ops:
  0.0 23.1 %shard_map.64 = bf16[1,256,1280]{2,1,0:T(8,128)(2,1)} custom-call(bf16[1,256,1280]{2,1,0:T(8,128)(2,1)} %tokens_hbm.1, bf16[16,1280]{1,0:T(8,128)(2,1)} %bitcast.1, bf16[1,1280,2560]{2,1,0:T(8,128)(2,1)} %w_in_hbm.1, bf16[1,5120]{1,0:T(2,128)(2,1)} %b_in_hbm.1, bf16[1,2560,1280]{2,1,0:T(8,128)(2,1)} %w_out_hbm.1, bf16[1,1280]{1,0:T(2,128)(2,1)} %b_out_hbm.1), custom_call_target="tpu_custom_call" | custom-call | tf_op jit(solution)/shard_map/pallas_call | solution.py:186
  23.1 2.0 %copy.8 = bf16[1,256,1280]{2,1,0:T(8,128)(2,1)} copy(bf16[1,256,1280]{2,1,0:T(8,128)(2,1)} %shard_map.64) | data formatting | bytes 1310720

commit v2 on v1

--- a/solution.py
+++ b/solution.py
@@ -16,25 +16,54 @@
     return v * (1.0 + lax.erf(v * (0.5**0.5))) * 0.5
 
 
-def exchange(n, n_ex, me, source, row_of, landing, send_sem, recv_sem):
-    def step(k, carry):
-        dest = lax.rem(me + k, n)
+def visit(n_dp, n_ex, me_dp, me_ex, action):
+    half = n_ex // 2
+    side = me_ex // half
+    inner = lax.rem(me_ex, half)
+    mirror = half - 1 - inner
+    crossing = (1 - side) * half
+    home = side * half
+
+    def run(count, step):
+        if count <= 8:
+            for j in range(count):
+                step(j)
+        else:
+            lax.fori_loop(0, count, lambda j, carry: step(j) or carry, 0)
+
+    def far(j):
+        for a in range(n_dp - 1, -1, -1):
+            action(lax.rem(me_dp + a, n_dp), crossing + lax.rem(mirror - j + half, half))
+
+    def near(j):
+        for a in range(n_dp - 1, -1, -1):
+            action(lax.rem(me_dp + a, n_dp), home + lax.rem(inner + 1 + j, half))
+
+    run(half, far)
+    run(half - 1, near)
+    for a in range(n_dp - 1, 0, -1):
+        action(lax.rem(me_dp + a, n_dp), me_ex)
+
+
+def exchange(n_dp, n_ex, me_dp, me_ex, source, row_of, landing, send_sem, recv_sem, chunks):
+    me = me_dp * n_ex + me_ex
+
+    def send(a, e):
         pltpu.make_async_remote_copy(
-            src_ref=source.at[row_of(dest)],
-            dst_ref=landing.at[me],
+            src_ref=source.at[row_of(a, e), pl.ds(0, chunks)],
+            dst_ref=landing.at[me, pl.ds(0, chunks)],
             send_sem=send_sem,
             recv_sem=recv_sem,
-            device_id=(dest // n_ex, lax.rem(dest, n_ex)),
+            device_id=(a, e),
             device_id_type=MESH,
         ).start()
-        return carry
-
-    lax.fori_loop(1, n, step, 0)
-    landing[me] = source[row_of(me)]
-
-
-def wait_bytes(buffer, count, sem):
-    rows = buffer.at[pl.ds(0, count)]
+
+    visit(n_dp, n_ex, me_dp, me_ex, send)
+    landing[me] = source[row_of(me_dp, me_ex)]
+
+
+def wait_bytes(buffer, count, chunks, sem):
+    rows = buffer.at[pl.ds(0, count), pl.ds(0, chunks)]
     pltpu.make_async_copy(rows, rows, sem).wait()
 
 
@@ -47,7 +76,8 @@
     b_in_hbm,
     w_out_hbm,
     b_out_hbm,
-    out_ref,
+    comb_ref,
+    eo,
     tok,
     router,
     w_in,
@@ -62,8 +92,6 @@
     recv2,
     x_ref,
     hid,
-    comb_ref,
-    eo,
     load_sems,
     w_in_sems,
     w_out_sems,
@@ -73,7 +101,6 @@
     n = n_dp * n_ex
     me_dp = lax.axis_index("dp")
     me_ex = lax.axis_index("expert")
-    me = me_dp * n_ex + me_ex
     width = tok.shape[1]
     chunks = width // LANES
     pitch = send1.shape[1]
@@ -84,19 +111,14 @@
         pltpu.make_async_copy(b_in_hbm, b_in, load_sems.at[2]),
         pltpu.make_async_copy(b_out_hbm, b_out, load_sems.at[3]),
     ]
-    for load in loads:
-        load.start()
-
+    loads[0].start()
+    loads[1].start()
     barrier = pltpu.get_barrier_semaphore()
 
-    def greet(k, carry):
-        dest = lax.rem(me + k, n)
-        pl.semaphore_signal(
-            barrier, inc=1, device_id=(dest // n_ex, lax.rem(dest, n_ex)), device_id_type=MESH
-        )
-        return carry
-
-    lax.fori_loop(1, n, greet, 0)
+    def greet(a, e):
+        pl.semaphore_signal(barrier, inc=1, device_id=(a, e), device_id_type=MESH)
+
+    visit(n_dp, n_ex, me_dp, me_ex, greet)
 
     def pieces(hbm, vmem, sems):
         count = sems.shape[0]
@@ -110,7 +132,7 @@
 
     w_in_loads = pieces(w_in_hbm, w_in, w_in_sems)
     w_out_loads = pieces(w_out_hbm, w_out, w_out_sems)
-    for load in w_in_loads + w_out_loads:
+    for load in w_in_loads + loads[2:] + w_out_loads:
         load.start()
 
     loads[0].wait()
@@ -126,7 +148,9 @@
     send1[...] = wide_slots[...].reshape(send1.shape).astype(jnp.bfloat16)
 
     pl.semaphore_wait(barrier, n - 1)
-    exchange(n, n_ex, me, send1, lambda d: lax.rem(d, n_ex), recv1, send_sems.at[0], recv_sems.at[0])
+    exchange(
+        n_dp, n_ex, me_dp, me_ex, send1, lambda a, e: e, recv1, send_sems.at[0], recv_sems.at[0], chunks
+    )
 
     over_experts = jnp.exp(logits - jnp.max(logits, axis=0, keepdims=True))
     combine = over_experts / jnp.sum(over_experts, axis=0, keepdims=True)
@@ -134,7 +158,7 @@
 
     for load in loads[2:] + w_in_loads:
         load.wait()
-    wait_bytes(recv1, n - 1, recv_sems.at[0])
+    wait_bytes(recv1, n - 1, chunks, recv_sems.at[0])
     wide_rows[...] = recv1[...].astype(jnp.float32).reshape(wide_rows.shape)
     for j in range(chunks):
         x_ref[:, j * LANES : (j + 1) * LANES] = wide_rows[pl.ds(j, n, stride=pitch), :].astype(jnp.bfloat16)
@@ -142,12 +166,10 @@
     half = w_in.shape[1]
     tile = 2 * LANES
 
-    @pl.loop(0, half // tile)
-    def _(t):
-        at = pl.multiple_of(t * tile, tile)
+    for at in range(0, half, tile):
         bias = b_in[:, pl.ds(pl.multiple_of(me_dp * half + at, LANES), tile)].astype(jnp.float32)
-        v = jnp.dot(x_ref[...], w_in[:, pl.ds(at, tile)], preferred_element_type=jnp.float32) + bias
-        hid[:, pl.ds(at, tile)] = gelu(v).astype(jnp.bfloat16)
+        v = jnp.dot(x_ref[...], w_in[:, at : at + tile], preferred_element_type=jnp.float32) + bias
+        hid[:, at : at + tile] = gelu(v).astype(jnp.bfloat16)
 
     for load in w_out_loads:
         load.wait()
@@ -159,20 +181,34 @@
             wide_rows[pl.ds(at // LANES + c, n, stride=pitch), :] = y[:, c * LANES : (c + 1) * LANES]
     send2[...] = wide_rows[...].reshape(send2.shape).astype(jnp.bfloat16)
 
-    exchange(n, n_ex, me, send2, lambda d: d, recv2, send_sems.at[1], recv_sems.at[1])
-    wait_bytes(recv2, n - 1, recv_sems.at[1])
+    exchange(
+        n_dp, n_ex, me_dp, me_ex, send2, lambda a, e: a * n_ex + e, recv2, send_sems.at[1], recv_sems.at[1], chunks
+    )
+    wait_bytes(recv2, n - 1, chunks, recv_sems.at[1])
     wide_rows[...] = recv2[...].astype(jnp.float32).reshape(wide_rows.shape)
     for j in range(chunks):
         total = wide_rows[pl.ds(j, n_ex, stride=pitch), :]
         for a in range(1, n_dp):
             total = total + wide_rows[pl.ds(a * n_ex * pitch + j, n_ex, stride=pitch), :]
         eo[:, j * LANES : (j + 1) * LANES] = total.astype(jnp.bfloat16)
-    mixed = lax.dot_general(
-        comb_ref[...], eo[...], (((0,), (0,)), ((), ())), preferred_element_type=jnp.float32
-    )
-    out_ref[0] = mixed.astype(jnp.bfloat16)
-    wait_bytes(recv1, n - 1, send_sems.at[0])
-    wait_bytes(recv2, n - 1, send_sems.at[1])
+    wait_bytes(recv1, n - 1, chunks, send_sems.at[0])
+    wait_bytes(recv2, n - 1, chunks, send_sems.at[1])
+
+
+def mix_kernel(combine, expert_out, out_hbm, mixed, sems):
+    count = sems.shape[0]
+    tile = mixed.shape[1] // count
+    writes = []
+    for i in range(count):
+        columns = pl.ds(i * tile, tile)
+        mixed[:, columns] = lax.dot_general(
+            combine[...], expert_out[:, columns], (((0,), (0,)), ((), ())), preferred_element_type=jnp.float32
+        ).astype(mixed.dtype)
+        write = pltpu.make_async_copy(mixed.at[:, columns], out_hbm.at[0, :, columns], sems.at[i])
+        write.start()
+        writes.append(write)
+    for write in writes:
+        write.wait()
 
 
 def shards(n_dp, n_ex, tokens, router, w_in, b_in, w_out, b_out):
@@ -183,11 +219,14 @@
     chunks = width // LANES
     pitch = -(-chunks // SUBLANES) * SUBLANES
     bf16, f32 = jnp.bfloat16, jnp.float32
-    return pl.pallas_call(
+    combine, expert_out = pl.pallas_call(
         functools.partial(kernel, n_dp, n_ex),
-        out_shape=jax.ShapeDtypeStruct(tokens.shape, bf16),
+        out_shape=[
+            pltpu.VMEM((n_ex, m), bf16),
+            pltpu.VMEM((n_ex, width), bf16),
+        ],
         in_specs=[pl.BlockSpec(memory_space=pltpu.HBM)] * 6,
-        out_specs=pl.BlockSpec(memory_space=pltpu.VMEM),
+        out_specs=[pl.BlockSpec(memory_space=pltpu.VMEM)] * 2,
         scratch_shapes=[
             pltpu.VMEM((m, width), bf16),
             pltpu.VMEM(router.shape[::-1], bf16),
@@ -203,8 +242,6 @@
             pltpu.VMEM((n, pitch, LANES), bf16),
             pltpu.VMEM((n, width), bf16),
             pltpu.VMEM((n, half), bf16),
-            pltpu.VMEM((n_ex, m), bf16),
-            pltpu.VMEM((n_ex, width), bf16),
             pltpu.SemaphoreType.DMA((4,)),
             pltpu.SemaphoreType.DMA((4,)),
             pltpu.SemaphoreType.DMA((4,)),
@@ -215,6 +252,18 @@
             collective_id=0, has_side_effects=True, vmem_limit_bytes=60 * 1024 * 1024
         ),
     )(tokens, router.T, w_in, b_in, w_out, b_out)
+    tile = 2 * LANES
+    return pl.pallas_call(
+        mix_kernel,
+        out_shape=jax.ShapeDtypeStruct(tokens.shape, bf16),
+        in_specs=[pl.BlockSpec(memory_space=pltpu.VMEM)] * 2,
+        out_specs=pl.BlockSpec(memory_space=pltpu.HBM),
+        scratch_shapes=[
+            pltpu.VMEM((m, width), bf16),
+            pltpu.SemaphoreType.DMA((width // tile,)),
+        ],
+        compiler_params=pltpu.CompilerParams(vmem_limit_bytes=8 * 1024 * 1024),
+    )(combine, expert_out)
 
 
 def solution(mesh):

time: 25.2 us -> 20 us (0.79)
  Pallas kernels: 23.1 us -> 19.9 us
  local copies, waits for them, and re-layouts: 1.97 us -> 0 us
    pallas_call x1 -> x2, Pallas kernels: 23.1 us -> 19.9 us  [the longest x1 18.7 us: shards(): pl.pallas_call(functools.partial(kernel, n_dp, n_ex), out_shape=[pltpu.VM...]
    unnamed x1 -> x0, local copies, waits for them, and re-layouts: 1.97 us -> none
where the time goes in v2:
time: 20 us; the launch traced here: 19.9 us
  Pallas kernels  19.9 us (99%)
    pallas_call x1, Pallas kernels, shards(): pl.pallas_call(functools.partial(kernel, n_dp, n_ex), out_shape=[pltpu.VM...  18.7 us
    pallas_call x1, Pallas kernels, shards(): pl.pallas_call(mix_kernel, out_shape=jax.ShapeDtypeStruct(tokens.shape, b...  1.12 us

profile of v2, /device:TPU:0, one launch (start us, length us, event | category | flops | bytes accessed | tf_op | source)
XLA Modules:
  0.0 19.9 jit_solution(17859011419077539923)
XLA Ops:
  0.0 18.7 %shard_map.64 = (bf16[16,256]{1,0:T(8,128)(2,1)S(1)}, bf16[16,1280]{1,0:T(8,128)(2,1)S(1)}) custom-call(bf16[1,256,1280]{2,1,0:T(8,128)(2,1)} %tokens_hbm.1, bf16[16,1280]{1,0:T(8,128)(2,1)} %bitcast.1, bf16[1,1280,2560]{2,1,0:T(8,128)(2,1)} %w_in_hbm.1, bf16[1,5120]{1,0:T(2,128)(2,1)} %b_in_hbm.1, bf16[1,2560,1280]{2,1,0:T(8,128)(2,1)} %w_out_hbm.1, ...), custom_call_target="tpu_custom_call" | custom-call | tf_op jit(solution)/shard_map/pallas_call | solution.py:222
  18.7 1.1 %shard_map.65 = bf16[1,256,1280]{2,1,0:T(8,128)(2,1)} custom-call(bf16[16,256]{1,0:T(8,128)(2,1)S(1)} %get-tuple-element.7.combine, bf16[16,1280]{1,0:T(8,128)(2,1)S(1)} %get-tuple-element.8.expert_out), custom_call_target="tpu_custom_call" | custom-call | tf_op jit(solution)/shard_map/pallas_call | solution.py:256

commit v3 on v2

--- a/solution.py
+++ b/solution.py
@@ -154,7 +154,7 @@
 
     over_experts = jnp.exp(logits - jnp.max(logits, axis=0, keepdims=True))
     combine = over_experts / jnp.sum(over_experts, axis=0, keepdims=True)
-    comb_ref[...] = combine.astype(jnp.bfloat16)
+    comb_ref[...] = combine.T.astype(jnp.bfloat16)
 
     for load in loads[2:] + w_in_loads:
         load.wait()
@@ -201,8 +201,8 @@
     writes = []
     for i in range(count):
         columns = pl.ds(i * tile, tile)
-        mixed[:, columns] = lax.dot_general(
-            combine[...], expert_out[:, columns], (((0,), (0,)), ((), ())), preferred_element_type=jnp.float32
+        mixed[:, columns] = jnp.dot(
+            combine[...], expert_out[:, columns], preferred_element_type=jnp.float32
         ).astype(mixed.dtype)
         write = pltpu.make_async_copy(mixed.at[:, columns], out_hbm.at[0, :, columns], sems.at[i])
         write.start()
@@ -222,7 +222,7 @@
     combine, expert_out = pl.pallas_call(
         functools.partial(kernel, n_dp, n_ex),
         out_shape=[
-            pltpu.VMEM((n_ex, m), bf16),
+            pltpu.VMEM((m, n_ex), bf16),
             pltpu.VMEM((n_ex, width), bf16),
         ],
         in_specs=[pl.BlockSpec(memory_space=pltpu.HBM)] * 6,

time: 20 us -> 19.9 us (level)
  no operation moved by 1% of the time
where the time goes in v3:
time: 19.9 us; the launch traced here: 19.8 us
  Pallas kernels  19.8 us (99%)
    pallas_call x1, Pallas kernels, shards(): pl.pallas_call(functools.partial(kernel, n_dp, n_ex), out_shape=[pltpu.VM...  18.7 us
    pallas_call x1, Pallas kernels, shards(): pl.pallas_call(mix_kernel, out_shape=jax.ShapeDtypeStruct(tokens.shape, b...  1.05 us

profile of v3, /device:TPU:0, one launch (start us, length us, event | category | flops | bytes accessed | tf_op | source)
XLA Modules:
  0.0 19.8 jit_solution(3488816161834132446)
XLA Ops:
  0.0 18.7 %shard_map.64 = (bf16[256,16]{1,0:T(8,128)(2,1)S(1)}, bf16[16,1280]{1,0:T(8,128)(2,1)S(1)}) custom-call(bf16[1,256,1280]{2,1,0:T(8,128)(2,1)} %tokens_hbm.1, bf16[16,1280]{1,0:T(8,128)(2,1)} %bitcast.1, bf16[1,1280,2560]{2,1,0:T(8,128)(2,1)} %w_in_hbm.1, bf16[1,5120]{1,0:T(2,128)(2,1)} %b_in_hbm.1, bf16[1,2560,1280]{2,1,0:T(8,128)(2,1)} %w_out_hbm.1, ...), custom_call_target="tpu_custom_call" | custom-call | tf_op jit(solution)/shard_map/pallas_call | solution.py:222
  18.7 1.1 %shard_map.65 = bf16[1,256,1280]{2,1,0:T(8,128)(2,1)} custom-call(bf16[256,16]{1,0:T(8,128)(2,1)S(1)} %get-tuple-element.7.combine, bf16[16,1280]{1,0:T(8,128)(2,1)S(1)} %get-tuple-element.8.expert_out), custom_call_target="tpu_custom_call" | custom-call | tf_op jit(solution)/shard_map/pallas_call | solution.py:256
